TPU v7x, 32 devices: a whole 2x2x4 slice. The times are simulated.
32 devices in a mesh: seq: 4 (over z), chan: 8 (over y, x, core).
Axes of the slice: x: 2, y: 2, z: 4, core: 2. Of those that a mesh axis runs over, the one named last changes fastest.
Arguments:
- tokens: bfloat16 [4096, 4096], P('seq', 'chan'), may hold values from -8 to 8
- norm_gain: float32 [4096], replicated, may hold values from 0.5 to 1.5
- gate_proj: bfloat16 [4096, 8192], P(None, 'chan'), may hold values from -0.09375 to 0.09375
- inner_proj: bfloat16 [4096, 8192], P(None, 'chan'), may hold values from -0.09375 to 0.09375
- state_proj: bfloat16 [4096, 384], P('chan'), may hold values from -0.11816406 to 0.11816406
- conv_inner: float32 [4, 8192], P(None, 'chan'), may hold values from -3 to 3
- conv_state: float32 [4, 256], replicated, may hold values from -3 to 3
- log_rate: float32 [128], P('chan'), may hold values from -1 to 0
- rate_bias: float32 [128], P('chan'), may hold values from -16 to -2
- skip_gain: float32 [128], P('chan'), may hold values from 0.2 to 4
- gate_gain: float32 [8192], P('chan'), may hold values from 0.5 to 1.5
- out_proj: bfloat16 [8192, 4096], P('chan'), may hold values from -0.09375 to 0.09375
Outputs:
- layer_out: bfloat16 [4096, 4096], P('seq', 'chan')
All inputs are finite; a program needn't handle non-finite values.
Results may differ from a plain program's by a relative error of at most 0.012.
Values may be sent and summed in bfloat16 or wider, within the bound.
A program may use at most 128 MiB of HBM per device.

v0:
```python
import jax
import jax.numpy as jnp
from jax import lax
from jax.sharding import PartitionSpec as P

P_SIZE = 64
N = 128
K = 4
Q = 256
DI = 8192


precise = lax.Precision.HIGHEST


def from_behind(value, axis, steps):
    count = lax.axis_size(axis)
    leading, last = (max(0, -steps), min(count, count - steps))
    return lax.ppermute(value, axis, [(source, source + steps) for source in range(leading, last)])


def causal_mix(rim_part, fresh_rows, weights):
    length = fresh_rows.shape[0]
    padded = jnp.concatenate([rim_part.astype(jnp.float32), fresh_rows.astype(jnp.float32)], axis=0)
    summed = jnp.zeros(fresh_rows.shape, jnp.float32)
    for offset in range(weights.shape[0]):
        summed = summed + weights[offset] * padded[offset : offset + length]
    return jax.nn.silu(summed)


def local(
    tokens,
    norm_gain,
    gate_proj,
    inner_proj,
    state_proj,
    conv_inner,
    conv_state,
    log_rate,
    rate_bias,
    skip_gain,
    gate_gain,
    out_proj,
):
    gathered = lax.all_gather(tokens, "chan", axis=1, tiled=True)
    widened = gathered.astype(jnp.float32)
    inverse = lax.rsqrt(jnp.mean(widened * widened, axis=1, keepdims=True) + 1e-05)
    normed = (widened * inverse * norm_gain).astype(jnp.bfloat16)
    gate_raw = jnp.dot(normed, gate_proj, preferred_element_type=jnp.float32).astype(jnp.bfloat16)
    inner_raw = jnp.dot(normed, inner_proj, preferred_element_type=jnp.float32).astype(jnp.bfloat16)
    heads = log_rate.shape[0]
    start_head = lax.axis_index("chan") * heads
    projected = jnp.dot(
        normed,
        lax.all_gather(state_proj, "chan", axis=0, tiled=True),
        preferred_element_type=jnp.float32,
    )
    state_raw = projected[:, : 2 * N]
    raw_rate = lax.dynamic_slice_in_dim(projected, 2 * N + start_head, heads, 1)
    rim_rows = from_behind(
        (inner_raw[-(K - 1) :].astype(jnp.float32), state_raw[-(K - 1) :]), "seq", 1
    )
    inner_conv = causal_mix(rim_rows[0].astype(jnp.bfloat16), inner_raw, conv_inner)
    state_conv = causal_mix(rim_rows[1], state_raw, conv_state)
    token_rows = tokens.shape[0]
    blocks = token_rows // Q
    step_size = jax.nn.softplus(raw_rate + rate_bias)
    decay_log = -jnp.exp(log_rate) * step_size
    values = inner_conv.reshape(blocks, Q, heads, P_SIZE)
    in_map = state_conv[:, :N].reshape(blocks, Q, N)
    out_map = state_conv[:, N:].reshape(blocks, Q, N)
    step_rows = step_size.reshape(blocks, Q, heads).transpose(0, 2, 1)
    log_rows = decay_log.reshape(blocks, Q, heads).transpose(0, 2, 1)
    lower_mask = (jnp.arange(Q)[:, None] >= jnp.arange(Q)[None, :]).astype(jnp.float32)
    within = jnp.einsum("chs,ts->cht", log_rows, lower_mask, precision=precise)
    log_gaps = within[..., :, None] - within[..., None, :]
    fading = jnp.exp(jnp.where(lower_mask > 0, log_gaps, -jnp.inf))
    scores = jnp.einsum("ctn,csn->cts", out_map, in_map, precision=precise)
    mixing = scores[:, None] * fading * step_rows[:, :, None, :]
    local_out = jnp.einsum("chts,cshp->cthp", mixing, values, precision=precise)
    tail_weight = jnp.exp(within[..., -1:] - within) * step_rows
    scaled = values * tail_weight.transpose(0, 2, 1)[..., None]
    block_end = jnp.einsum("csn,cshp->chnp", in_map, scaled, precision=precise)
    block_log = within[..., -1]
    through = jnp.cumsum(block_log, axis=0)
    before = through - block_log
    earlier = jnp.arange(blocks)[:, None] > jnp.arange(blocks)[None, :]
    passage = jnp.exp(
        jnp.where(earlier[:, :, None], before[:, None, :] - through[None, :, :], -jnp.inf)
    )
    entering = jnp.einsum("cdh,dhnp->chnp", passage, block_end, precision=precise)
    device_end = jnp.einsum(
        "ch,chnp->hnp", jnp.exp(through[-1:] - through), block_end, precision=precise
    )
    device_fade = jnp.exp(through[-1])

    def hand_on(turn_index, incoming):
        return from_behind(device_fade[:, None, None] * incoming + device_end, "seq", 1)

    carried = lax.fori_loop(0, lax.axis_size("seq") - 1, hand_on, jnp.zeros_like(device_end))
    entering = entering + jnp.exp(before)[:, :, None, None] * carried[None]
    carried_out = jnp.einsum("ctn,chnp->cthp", out_map, entering, precision=precise)
    carried_out = carried_out * jnp.exp(within).transpose(0, 2, 1)[..., None]
    skip_wide = jnp.repeat(skip_gain, P_SIZE)
    ssd_out = (local_out + carried_out).reshape(token_rows, heads * P_SIZE) + skip_wide * inner_conv
    gated_out = ssd_out * jax.nn.silu(gate_raw.astype(jnp.float32))
    energy = lax.psum(jnp.sum(gated_out * gated_out, axis=1), "chan")
    norm_scale = lax.rsqrt(energy / DI + 1e-05)
    shaped = (gated_out * norm_scale[:, None] * gate_gain).astype(jnp.bfloat16)
    partial_out = jnp.dot(shaped, out_proj, preferred_element_type=jnp.float32)
    summed = lax.psum_scatter(partial_out, "chan", scatter_dimension=1, tiled=True)
    return (tokens.astype(jnp.float32) + summed).astype(jnp.bfloat16)


def solution(mesh):
    return jax.shard_map(
        local,
        mesh=mesh,
        in_specs=(
            P("seq", "chan"),
            P(),
            P(None, "chan"),
            P(None, "chan"),
            P("chan", None),
            P(None, "chan"),
            P(),
            P("chan"),
            P("chan"),
            P("chan"),
            P("chan"),
            P("chan", None),
        ),
        out_specs=P("seq", "chan"),
        check_vma=False,
    )
```

profile of v0, /device:TPU:0, one launch (start us, length us, event | category | flops | bytes accessed | tf_op | source)
XLA Modules:
  0.0 421.3 jit_solution(6865665323999386071)
XLA Ops:
  10.4 0.9 fusion.71
  11.3 56.5 %all-gather.3.cloned.1.call-done = bf16[1024,4096]{1,0:T(8,128)(2,1)} async-done(((bf16[1024,512]{1,0:T(8,128)(2,1)}), bf16[1024,4096]{1,0:T(8,128)(2,1)}) %all-gather.3.cloned.1.call-update) | async-done | bytes 8388624 | tf_op jit(solution)/shard_map/all_gather | solution.py:45
  67.8 5.1 %fusion = f32[1024]{0:T(1024)S(1)} fusion(bf16[1024,4096]{1,0:T(8,128)(2,1)} %all-gather.3.cloned.1.call-done), kind=kLoop, calls=%fused_computation.3 | loop fusion | flops 12581888 | bytes 8392704 | tf_op jit(solution)/shard_map/reduce_sum | solution.py:47
  72.9 29.0 %all-gather.5.cloned.1.call-done = bf16[4096,384]{1,0:T(8,128)(2,1)} async-done(((bf16[512,384]{1,0:T(8,128)(2,1)}), bf16[4096,384]{1,0:T(8,128)(2,1)}) %all-gather.5.cloned.1.call-update) | async-done | bytes 3145744 | tf_op jit(solution)/shard_map/all_gather | solution.py:55
  101.9 8.1 %fusion.66 = f32[1024,384]{1,0:T(8,128)S(1)} fusion(bf16[4096,384]{1,0:T(8,128)(2,1)} %all-gather.5.cloned.1.call-done, bf16[1024,4096]{1,0:T(8,128)(2,1)} %all-gather.3.cloned.1.call-done, f32[4096]{0:T(1024)S(1)} %copy-done.4, f32[1024]{0:T(1024)S(1)} %add_rsqrt_fusion.1), kind=kOutput, calls=%fused_computation.96 | convolution fusion | flops 3238002688 | bytes 13127680 | tf_op jit(solution)/shard_map/dot_general | solution.py:53
  111.4 15.2 %fusion.73 = (f32[1024,1024]{1,0:T(8,128)}, bf16[1024,1024]{1,0:T(8,128)(2,1)S(1)}) fusion(bf16[4096,1024]{1,0:T(8,128)(2,1)} %param.17, bf16[1024,4096]{1,0:T(8,128)(2,1)} %all-gather.3.cloned.1.call-done, f32[4096]{0:T(1024)S(1)} %copy-done.4, f32[1024]{0:T(1024)S(1)} %add_rsqrt_fusion.1), kind=kOutput, calls=%fused_computation.101 | convolution fusion | flops 8608808960 | bytes 23089152 | tf_op jit(solution)/shard_map/dot_general | solution.py:50
  126.6 3.4 collective-permute-start.1
  130.0 3.6 collective-permute-start.2
  133.8 0.9 collective-permute-done.2
  135.4 1.0 fusion.74
  136.5 3.9 divide_multiply_fusion
  140.3 5.3 %copy.47 = f32[1024,1024]{0,1:T(8,128)} copy(f32[1024,1024]{1,0:T(8,128)} %divide_multiply_fusion) | data formatting | bytes 8388608 | tf_op jit(solution)/shard_map/jit(silu)/mul | solution.py:28
  145.7 5.6 %reshape.68 = f32[4,256,16,64]{1,0,3,2:T(4,128)} reshape(f32[1024,1024]{0,1:T(8,128)} %copy.47) | data formatting | bytes 8388608 | tf_op jit(solution)/shard_map/reshape | solution.py:69
  151.3 3.3 broadcast_multiply_fusion
  154.7 5.4 %fusion.31 = (f32[16,128,64]{1,2,0:T(8,128)S(1)}, f32[4,16,64,128]{3,2,1,0:T(8,128)}) fusion(f32[16,4]{0,1:T(4,128)S(1)} %get-tuple-element.50, f32[4,256,128,1]{2,1,3,0:T(8,128)S(1)} %bitcast.77, f32[4,256,16,64]{1,0,3,2:T(4,128)S(1)} %broadcast_multiply_fusion), kind=kOutput, calls=%fused_computation.44 | convolution fusion | flops 1611530240 | bytes 7340288 | tf_op jit(solution)/shard_map/csn,cshp->chnp/dot_general | solution.py:83
  160.1 41.4 %while.10 = (s32[]{:T(128)}, f32[16,128,64]{1,2,0:T(8,128)S(1)}, f32[16]{0:T(128)S(1)}, f32[16,128,64]{1,2,0:T(8,128)S(1)}, s32[]{:T(128)}) while((s32[]{:T(128)}, f32[16,128,64]{1,2,0:T(8,128)S(1)}, f32[16]{0:T(128)S(1)}, f32[16,128,64]{1,2,0:T(8,128)S(1)}, s32[]{:T(128)}) %tuple.31), condition=%wide.region_3.4_spmd, body=%wide.region_2.3_spmd.sunk | while | flops 262146 | bytes 3670181 | solution.py:100
  160.3 4.2 %collective-permute-start = (f32[16,128,64]{1,2,0:T(8,128)S(1)}, f32[16,128,64]{1,2,0:T(8,128)S(1)}, u32[]{:S(2)}, u32[]{:S(2)}) collective-permute-start(f32[16,128,64]{1,2,0:T(8,128)S(1)} %multiply_add_fusion.2), channel_id=1, source_target_pairs={{0,8},{8,16},{16,24},{1,9},{9,17},{17,25},{2,10},{10,18},{18,26},{... | collective-permute-start | bytes 1572872 | tf_op jit(solution)/shard_map/while/body/eval_jaxpr/ppermute | solution.py:19
  164.5 10.1 %collective-permute-done = f32[16,128,64]{1,2,0:T(8,128)S(1)} collective-permute-done((f32[16,128,64]{1,2,0:T(8,128)S(1)}, f32[16,128,64]{1,2,0:T(8,128)S(1)}, u32[]{:S(2)}, u32[]{:S(2)}) %collective-permute-start) | collective-permute-done | bytes 524320 | tf_op jit(solution)/shard_map/while/body/eval_jaxpr/ppermute | solution.py:19
  174.7 4.4 %collective-permute-start = (f32[16,128,64]{1,2,0:T(8,128)S(1)}, f32[16,128,64]{1,2,0:T(8,128)S(1)}, u32[]{:S(2)}, u32[]{:S(2)}) collective-permute-start(f32[16,128,64]{1,2,0:T(8,128)S(1)} %multiply_add_fusion.2), channel_id=1, source_target_pairs={{0,8},{8,16},{16,24},{1,9},{9,17},{17,25},{2,10},{10,18},{18,26},{... | collective-permute-start | bytes 1572872 | tf_op jit(solution)/shard_map/while/body/eval_jaxpr/ppermute | solution.py:19
  179.2 9.3 %collective-permute-done = f32[16,128,64]{1,2,0:T(8,128)S(1)} collective-permute-done((f32[16,128,64]{1,2,0:T(8,128)S(1)}, f32[16,128,64]{1,2,0:T(8,128)S(1)}, u32[]{:S(2)}, u32[]{:S(2)}) %collective-permute-start) | collective-permute-done | bytes 524320 | tf_op jit(solution)/shard_map/while/body/eval_jaxpr/ppermute | solution.py:19
  188.5 4.4 %collective-permute-start = (f32[16,128,64]{1,2,0:T(8,128)S(1)}, f32[16,128,64]{1,2,0:T(8,128)S(1)}, u32[]{:S(2)}, u32[]{:S(2)}) collective-permute-start(f32[16,128,64]{1,2,0:T(8,128)S(1)} %multiply_add_fusion.2), channel_id=1, source_target_pairs={{0,8},{8,16},{16,24},{1,9},{9,17},{17,25},{2,10},{10,18},{18,26},{... | collective-permute-start | bytes 1572872 | tf_op jit(solution)/shard_map/while/body/eval_jaxpr/ppermute | solution.py:19
  193.0 8.4 %collective-permute-done = f32[16,128,64]{1,2,0:T(8,128)S(1)} collective-permute-done((f32[16,128,64]{1,2,0:T(8,128)S(1)}, f32[16,128,64]{1,2,0:T(8,128)S(1)}, u32[]{:S(2)}, u32[]{:S(2)}) %collective-permute-start) | collective-permute-done | bytes 524320 | tf_op jit(solution)/shard_map/while/body/eval_jaxpr/ppermute | solution.py:19
  201.6 6.7 %bitcast_add_fusion.1 = f32[4,16,128,64]{2,0,3,1:T(4,128)S(1)} fusion(f32[4,16,128,64]{2,3,1,0:T(8,128)} %bitcast.72, f32[16,128,64]{1,2,0:T(8,128)S(1)} %get-tuple-element.27, f32[4,16]{0,1:T(8,128)S(1)} %copy.58, f32[4,16]{0,1:T(8,128)S(1)} %copy.56, f32[4,16]{0,1:T(8,128)S(1)} %copy.55, pred[4,4]{1,0:T(4,128)(4,1)S(1)} %iota_compare_fusion.1), kind=kOutput, calls=%fused_computation.45 | convolution fusion | flops 26214912 | bytes 4719376 | tf_op jit(solution)/shard_map/cdh,dhnp->chnp/dot_general | solution.py:91
  208.6 3.5 fusion.75
  212.1 20.6 %bitcast_add_fusion = f32[4,256,16,64]{1,3,2,0:T(8,128)} fusion(f32[4,256,16,64]{1,3,2,0:T(8,128)S(1)} %bitcast.78, f32[4,256,16]{1,2,0:T(8,128)S(1)} %exponential_bitcast_fusion, f32[4,16,256]{2,1,0:T(8,128)S(1)} %copy.50, f32[4,16,256]{2,1,0:T(8,128)S(1)} %fusion.51, f32[4,256,256]{2,1,0:T(8,128)S(1)} %fusion.74, ...), kind=kOutput, calls=%fused_computation.35 | convolution fusion | flops 3240099840 | bytes 13893632 | tf_op jit(solution)/shard_map/chts,cshp->cthp/dot_general | solution.py:80
  232.7 8.1 %copy.71 = f32[4,256,16,64]{3,2,1,0:T(8,128)} copy(f32[4,256,16,64]{1,3,2,0:T(8,128)} %bitcast_add_fusion) | data formatting | bytes 8388608 | tf_op jit(solution)/shard_map/reshape | solution.py:105
  240.7 7.7 %reshape.81 = f32[1024,1024]{1,0:T(8,128)} reshape(f32[4,256,16,64]{3,2,1,0:T(8,128)} %copy.71) | data formatting | bytes 8388608 | tf_op jit(solution)/shard_map/reshape | solution.py:105
  248.4 18.5 %multiply_reduce_fusion = (f32[1024]{0:T(1024)S(1)}, f32[1024,1024]{1,0:T(8,128)}) fusion(bf16[4096,1024]{1,0:T(8,128)(2,1)} %param.16, bf16[1024,4096]{1,0:T(8,128)(2,1)} %all-gather.3.cloned.1.call-done, f32[4096]{0:T(1024)S(1)} %copy-done.4, f32[1024]{0:T(1024)S(1)} %add_rsqrt_fusion.1, f32[1024,1024]{1,0:T(8,128)} %reshape.81, ...), kind=kOutput, calls=%fused_computation.40 | convolution fusion | flops 8618245120 | bytes 29388800 | tf_op jit(solution)/shard_map/dot_general | solution.py:49
  266.9 11.8 %psum.7 = f32[1024]{0:T(1024)S(1)} all-reduce(f32[1024]{0:T(1024)S(1)} %get-tuple-element.55), channel_id=1, replica_groups=mesh['seq'=4,'chan'=8] {'chan'}, use_global_device_ids=true, to_apply=%region_5.6 | all-reduce | flops 1024 | bytes 8192 | tf_op jit(solution)/shard_map/psum | solution.py:107
  278.7 16.2 %fusion.30 = f32[1024,4096]{1,0:T(8,128)} fusion(bf16[1024,4096]{1,0:T(8,128)(2,1)} %param.25, f32[1024,1024]{1,0:T(8,128)} %get-tuple-element.56, f32[1024]{0:T(1024)S(1)} %copy-done.5, f32[1024]{0:T(1024)S(1)} %add_rsqrt_fusion), kind=kOutput, calls=%fused_computation.42 | convolution fusion | flops 8593080320 | bytes 29368320 | tf_op jit(solution)/shard_map/dot_general | solution.py:110
  294.9 116.4 %reduce-scatter.2.cloned.1.call-done = f32[1024,512]{1,0:T(8,128)} async-done(((f32[1024,4096]{1,0:T(8,128)}), f32[1024,512]{1,0:T(8,128)}) %reduce-scatter.2.cloned.1.call-update) | async-done | bytes 2097168 | tf_op jit(solution)/shard_map/reduce_scatter | solution.py:111
  411.4 2.9 add_convert_fusion
  (55 shorter events, 6.8 us)
Async XLA Ops:
  6.5 61.3 %all-gather.3.cloned.1.call-start = ((), (), s32[]{:S(2)}) async-start(), calls=%async_computation.1 | async-start | bytes 9437184 | tf_op jit(solution)/shard_map/all_gather | solution.py:45
  7.3 94.7 %all-gather.5.cloned.1.call-start = ((), (), s32[]{:S(2)}) async-start(), calls=%async_computation.2 | async-start | bytes 3538944 | tf_op jit(solution)/shard_map/all_gather | solution.py:55
  8.0 403.4 %reduce-scatter.2.cloned.1.call-start = ((), (), s32[]{:S(2)}) async-start(), calls=%async_computation.3 | async-start | bytes 18874368 | tf_op jit(solution)/shard_map/reduce_scatter | solution.py:111
  11.3 90.6 %copy-start.4 = (f32[4096]{0:T(1024)S(1)}, f32[4096]{0:T(1024)}, u32[]{:S(2)}) copy-start(f32[4096]{0:T(1024)} %param.15) | copy-start | bytes 49156
  72.9 37.6 %copy-start.3 = (f32[16]{0:T(128)S(1)}, f32[16]{0:T(128)}, u32[]{:S(2)}) copy-start(f32[16]{0:T(128)} %param.22) | copy-start | bytes 196
  126.6 9.8 %collective-permute-start.1 = (bf16[3,1024]{1,0:T(4,128)(2,1)S(1)}, bf16[3,1024]{1,0:T(4,128)(2,1)S(1)}, u32[]{:S(2)}, u32[]{:S(2)}) collective-permute-start(bf16[3,1024]{1,0:T(4,128)(2,1)S(1)} %slice.162), channel_id=1, source_target_pairs={{0,8},{8,16},{16,24},{1,9},{9,17},{17,25},{2,10},{10,18},{18,26},{... | collective-permute-start | bytes 18440 | tf_op jit(solution)/shard_map/ppermute | solution.py:19
  130.0 4.7 %collective-permute-start.2 = (f32[3,256]{1,0:T(4,128)S(1)}, f32[3,256]{1,0:T(4,128)S(1)}, u32[]{:S(2)}, u32[]{:S(2)}) collective-permute-start(f32[3,256]{1,0:T(4,128)S(1)} %slice.92), channel_id=1, source_target_pairs={{0,8},{8,16},{16,24},{1,9},{9,17},{17,25},{2,10},{10,18},{18,26},{... | collective-permute-start | bytes 9224 | tf_op jit(solution)/shard_map/ppermute | solution.py:19
  133.8 2.7 copy-start.1
  160.3 14.3 %collective-permute-start = (f32[16,128,64]{1,2,0:T(8,128)S(1)}, f32[16,128,64]{1,2,0:T(8,128)S(1)}, u32[]{:S(2)}, u32[]{:S(2)}) collective-permute-start(f32[16,128,64]{1,2,0:T(8,128)S(1)} %multiply_add_fusion.2), channel_id=1, source_target_pairs={{0,8},{8,16},{16,24},{1,9},{9,17},{17,25},{2,10},{10,18},{18,26},{... | collective-permute-start | bytes 1572872 | tf_op jit(solution)/shard_map/while/body/eval_jaxpr/ppermute | solution.py:19
  174.7 13.7 %collective-permute-start = (f32[16,128,64]{1,2,0:T(8,128)S(1)}, f32[16,128,64]{1,2,0:T(8,128)S(1)}, u32[]{:S(2)}, u32[]{:S(2)}) collective-permute-start(f32[16,128,64]{1,2,0:T(8,128)S(1)} %multiply_add_fusion.2), channel_id=1, source_target_pairs={{0,8},{8,16},{16,24},{1,9},{9,17},{17,25},{2,10},{10,18},{18,26},{... | collective-permute-start | bytes 1572872 | tf_op jit(solution)/shard_map/while/body/eval_jaxpr/ppermute | solution.py:19
  188.5 12.8 %collective-permute-start = (f32[16,128,64]{1,2,0:T(8,128)S(1)}, f32[16,128,64]{1,2,0:T(8,128)S(1)}, u32[]{:S(2)}, u32[]{:S(2)}) collective-permute-start(f32[16,128,64]{1,2,0:T(8,128)S(1)} %multiply_add_fusion.2), channel_id=1, source_target_pairs={{0,8},{8,16},{16,24},{1,9},{9,17},{17,25},{2,10},{10,18},{18,26},{... | collective-permute-start | bytes 1572872 | tf_op jit(solution)/shard_map/while/body/eval_jaxpr/ppermute | solution.py:19
  208.6 3.5 copy-start
  248.4 30.3 %copy-start.5 = (f32[1024]{0:T(1024)S(1)}, f32[1024]{0:T(1024)}, u32[]{:S(2)}) copy-start(f32[1024]{0:T(1024)} %param.24) | copy-start | bytes 12292
  294.9 116.5 %copy-start.2 = (bf16[1024,512]{1,0:T(8,128)(2,1)S(1)}, bf16[1024,512]{1,0:T(8,128)(2,1)}, u32[]{:S(2)}) copy-start(bf16[1024,512]{1,0:T(8,128)(2,1)} %param.14) | copy-start | bytes 3145732
Sparse Core Ops, SparseCore 0:
  9.2 58.5 all-gather.2
  69.7 32.1 all-gather.4
  295.0 116.2 reduce-scatter.1
where the time goes:
time: 429 us; the launch traced here: 421 us
  waiting for transfers between devices  232 us (54%)
  matrix products  95.5 us (22%)
  local copies, waits for them, and re-layouts  30.6 us (7%)
  starting transfers between devices  20.1 us (5%)
  other arithmetic  17.1 us (4%)
  between operations  13.9 us (3%)
  blocking collectives  11.8 us (3%)
    reduce_scatter x1, waiting for transfers between devices, local(): lax.psum_scatter(partial_out, 'chan', scatter_dimension=1, tiled=True)  116 us
    all_gather x1, waiting for transfers between devices, local(): gathered = lax.all_gather(tokens, 'chan', axis=1, tiled=True)  56.5 us
    all_gather x1, waiting for transfers between devices, local(): lax.all_gather(state_proj, 'chan', axis=0, tiled=True)  29 us
    ppermute x5, waiting for transfers between devices, from_behind(): lax.ppermute(value, axis, [(source, source + steps) for source in range(l...  28.7 us
    dot_general x1, matrix products, local(): local_out = jnp.einsum('chts,cshp->cthp', mixing, values, precision=precise)  20.6 us
    ppermute x5, starting transfers between devices, from_behind(): lax.ppermute(value, axis, [(source, source + steps) for source in range(l...  20 us
    dot_general x1, matrix products, local(): jnp.dot(normed, gate_proj, preferred_element_type=jnp.float32)  18.5 us
    dot_general x1, matrix products, local(): partial_out = jnp.dot(shaped, out_proj, preferred_element_type=jnp.float32)  16.2 us
  transfers between devices with their start and end apart: 8, of which 7 were waited for; matrix products, arithmetic and copies ran while one was open for 2% of the time, Pallas kernels for 0%

commit v1 on v0

v1 whole, which is shorter than its diff:
```python
import jax
import jax.numpy as jnp
from jax import lax
from jax.experimental import pallas as pl
from jax.experimental.pallas import tpu as pltpu
from jax.sharding import PartitionSpec as P

P_SIZE = 64
N = 128
K = 4
Q = 256
LANES = 2 * P_SIZE
RIM = 8

f32, bf16 = jnp.float32, jnp.bfloat16


def from_behind(value, axis, steps):
    count = lax.axis_size(axis)
    leading, last = (max(0, -steps), min(count, count - steps))
    return lax.ppermute(value, axis, [(source, source + steps) for source in range(leading, last)])


def wide_pair(columns, pair):
    rows = columns.shape[0]
    lane = lax.broadcasted_iota(jnp.int32, (rows, LANES), 1)
    first = jnp.broadcast_to(columns[:, 2 * pair : 2 * pair + 1], (rows, LANES))
    second = jnp.broadcast_to(columns[:, 2 * pair + 1 : 2 * pair + 2], (rows, LANES))
    return jnp.where(lane < P_SIZE, first, second)


def scan_kernel(
    inner_ref, inner_rim_ref, state_ref, state_rim_ref, step_ref, step_t_ref, rate_ref, rate_t_ref,
    conv_inner_ref, conv_state_ref, skip_ref,
    y_ref, out_map_ref, log_ref, end_ref, fade_ref,
    held, state_ext, inner_ext, total,
):
    block = pl.program_id(0)
    heads = step_ref.shape[1]

    @pl.when(block == 0)
    def _():
        held[...] = jnp.zeros_like(held)
        total[...] = jnp.zeros_like(total)
        state_ext[0:RIM] = state_rim_ref[...]
        inner_ext[0:RIM] = inner_rim_ref[...]

    state_ext[RIM : RIM + Q] = state_ref[...]
    inner_ext[RIM : RIM + Q] = inner_ref[...].astype(f32)

    def mixed(ext, taps, lanes):
        summed = taps[0:1, lanes] * ext[RIM - 3 : RIM - 3 + Q, lanes]
        for offset in range(1, K):
            start = RIM - (K - 1) + offset
            summed = summed + taps[offset : offset + 1, lanes] * ext[start : start + Q, lanes]
        return summed * (1.0 / (1.0 + jnp.exp(-summed)))

    in_map = mixed(state_ext, conv_state_ref, slice(0, N))
    out_map = mixed(state_ext, conv_state_ref, slice(N, 2 * N)).astype(bf16)
    out_map_ref[...] = out_map
    in_map_t = jnp.transpose(in_map).astype(bf16)

    row = lax.broadcasted_iota(jnp.int32, (Q, Q), 0)
    column = lax.broadcasted_iota(jnp.int32, (Q, Q), 1)
    lower = row >= column
    scores = jnp.dot(out_map, in_map_t, preferred_element_type=f32)
    scores = jnp.where(lower, scores, 0.0)
    step = step_ref[...]
    logs = rate_ref[...] * step
    logs_t = rate_t_ref[...] * step_t_ref[...]
    within = jnp.dot(
        lower.astype(f32), logs, precision=lax.Precision.HIGHEST, preferred_element_type=f32
    )
    within_t = jnp.dot(
        logs_t, (row <= column).astype(f32), precision=lax.Precision.HIGHEST,
        preferred_element_type=f32,
    )
    log_ref[...] = within + total[...]
    last = within[Q - 1 : Q]
    grown = jnp.exp(within)
    tail = jnp.exp(last - within) * step
    block_fade = jnp.exp(last)
    lane = lax.broadcasted_iota(jnp.int32, (Q, LANES), 1)
    for pair in range(heads // 2):
        lanes = slice(pair * LANES, (pair + 1) * LANES)
        x = mixed(inner_ext, conv_inner_ref, lanes)
        stepped = (x * wide_pair(step, pair)).astype(bf16)
        parts = []
        for head in (2 * pair, 2 * pair + 1):
            gap = within[:, head : head + 1] - within_t[head : head + 1, :]
            mixing = (scores * jnp.exp(jnp.minimum(gap, 0.0))).astype(bf16)
            parts.append(jnp.dot(mixing, stepped, preferred_element_type=f32))
        inside = jnp.where(lane < P_SIZE, parts[0], parts[1])
        before = held[:, lanes]
        carried = jnp.dot(out_map, before.astype(bf16), preferred_element_type=f32)
        y_ref[:, lanes] = inside + carried * wide_pair(grown, pair) + skip_ref[:, lanes] * x
        tailed = (x * wide_pair(tail, pair)).astype(bf16)
        fresh = jnp.dot(in_map_t, tailed, preferred_element_type=f32)
        held[:, lanes] = wide_pair(block_fade, pair) * before + fresh
    total[...] = total[...] + last
    end_ref[...] = held[...]
    fade_ref[...] = jnp.exp(total[...])
    state_ext[0:RIM] = state_ext[Q : Q + RIM]
    inner_ext[0:RIM] = inner_ext[Q : Q + RIM]


def local_scan(inner_raw, inner_rim, state_raw, state_rim, step, rate, conv_inner, conv_state, skip_wide):
    rows, width = inner_raw.shape
    heads = step.shape[1]

    def whole(shape):
        return pl.BlockSpec(shape, lambda c: (0, 0))

    return pl.pallas_call(
        scan_kernel,
        grid=(rows // Q,),
        in_specs=[
            pl.BlockSpec((Q, width), lambda c: (c, 0)),
            whole((RIM, width)),
            pl.BlockSpec((Q, 2 * N), lambda c: (c, 0)),
            whole((RIM, 2 * N)),
            pl.BlockSpec((Q, heads), lambda c: (c, 0)),
            pl.BlockSpec((heads, Q), lambda c: (0, c)),
            whole((1, heads)),
            whole((heads, 1)),
            whole((K, width)),
            whole((K, 2 * N)),
            whole((1, width)),
        ],
        out_specs=[
            pl.BlockSpec((Q, width), lambda c: (c, 0)),
            pl.BlockSpec((Q, N), lambda c: (c, 0)),
            pl.BlockSpec((Q, heads), lambda c: (c, 0)),
            whole((N, width)),
            whole((1, heads)),
        ],
        out_shape=[
            jax.ShapeDtypeStruct((rows, width), f32),
            jax.ShapeDtypeStruct((rows, N), bf16),
            jax.ShapeDtypeStruct((rows, heads), f32),
            jax.ShapeDtypeStruct((N, width), f32),
            jax.ShapeDtypeStruct((1, heads), f32),
        ],
        scratch_shapes=[
            pltpu.VMEM((N, width), f32),
            pltpu.VMEM((RIM + Q, 2 * N), f32),
            pltpu.VMEM((RIM + Q, width), f32),
            pltpu.VMEM((1, heads), f32),
        ],
        compiler_params=pltpu.CompilerParams(dimension_semantics=("arbitrary",)),
        cost_estimate=pl.CostEstimate(
            flops=rows * width * Q * 4, bytes_accessed=rows * width * 8, transcendentals=rows * heads * Q
        ),
    )(
        inner_raw, inner_rim, state_raw, state_rim, step, step.T, rate[None, :], rate[:, None],
        conv_inner, conv_state, skip_wide,
    )


def finish_kernel(y_ref, gate_ref, out_map_ref, log_ref, carried_ref, gain_ref, shaped_ref, energy_ref):
    heads = log_ref.shape[1]
    grown = jnp.exp(log_ref[...])
    out_map = out_map_ref[...]
    energy = jnp.zeros((Q, LANES), f32)
    for pair in range(heads // 2):
        lanes = slice(pair * LANES, (pair + 1) * LANES)
        carried = jnp.dot(out_map, carried_ref[:, lanes], preferred_element_type=f32)
        y = y_ref[:, lanes] + carried * wide_pair(grown, pair)
        gate = gate_ref[:, lanes].astype(f32)
        gated = y * (gate * (1.0 / (1.0 + jnp.exp(-gate))))
        energy = energy + gated * gated
        shaped_ref[:, lanes] = (gated * gain_ref[:, lanes]).astype(bf16)
    energy_ref[...] = jnp.sum(energy, axis=1, keepdims=True)


def finish(y, gate_raw, out_map, logs, carried, gate_gain):
    rows, width = y.shape
    heads = logs.shape[1]

    def rowwise(columns):
        return pl.BlockSpec((Q, columns), lambda c: (c, 0))

    return pl.pallas_call(
        finish_kernel,
        grid=(rows // Q,),
        in_specs=[
            rowwise(width),
            rowwise(width),
            rowwise(N),
            rowwise(heads),
            pl.BlockSpec((N, width), lambda c: (0, 0)),
            pl.BlockSpec((1, width), lambda c: (0, 0)),
        ],
        out_specs=[rowwise(width), rowwise(1)],
        out_shape=[
            jax.ShapeDtypeStruct((rows, width), bf16),
            jax.ShapeDtypeStruct((rows, 1), f32),
        ],
        compiler_params=pltpu.CompilerParams(dimension_semantics=("arbitrary",)),
        cost_estimate=pl.CostEstimate(
            flops=rows * width * N * 2, bytes_accessed=rows * width * 8, transcendentals=rows * width
        ),
    )(y, gate_raw, out_map, logs, carried, gate_gain)


def local(
    tokens,
    norm_gain,
    gate_proj,
    inner_proj,
    state_proj,
    conv_inner,
    conv_state,
    log_rate,
    rate_bias,
    skip_gain,
    gate_gain,
    out_proj,
):
    token_rows = tokens.shape[0]
    together = jnp.concatenate([tokens, state_proj.T], axis=0)
    together = lax.all_gather(together, "chan", axis=1, tiled=True)
    gathered, state_proj_t = together[:token_rows], together[token_rows:]
    widened = gathered.astype(f32)
    inverse = lax.rsqrt(jnp.mean(widened * widened, axis=1, keepdims=True) + 1e-05)
    normed = (widened * inverse * norm_gain).astype(bf16)
    projected = lax.dot_general(
        normed, state_proj_t, (((1,), (1,)), ((), ())), preferred_element_type=f32
    )
    inner_raw = jnp.dot(normed, inner_proj, preferred_element_type=f32).astype(bf16)
    gate_raw = jnp.dot(normed, gate_proj, preferred_element_type=f32).astype(bf16)
    heads = log_rate.shape[0]
    start_head = lax.axis_index("chan") * heads
    state_raw = projected[:, : 2 * N]
    raw_rate = lax.dynamic_slice_in_dim(projected, 2 * N + start_head, heads, 1)
    step = jax.nn.softplus(raw_rate + rate_bias)
    inner_rim = from_behind(inner_raw[-RIM:], "seq", 1).astype(f32)
    state_rim = from_behind(state_raw[-RIM:], "seq", 1)
    skip_wide = jnp.repeat(skip_gain, P_SIZE)[None, :]
    y, out_map, logs, device_end, device_fade = local_scan(
        inner_raw, inner_rim, state_raw, state_rim, step, -jnp.exp(log_rate),
        conv_inner, conv_state, skip_wide,
    )
    fade_wide = jnp.repeat(device_fade[0], P_SIZE)[None, :]
    carried = from_behind(device_end.astype(bf16), "seq", 1)
    for _ in range(lax.axis_size("seq") - 2):
        carried = from_behind((fade_wide * carried.astype(f32) + device_end).astype(bf16), "seq", 1)
    shaped, energy = finish(y, gate_raw, out_map, logs, carried, gate_gain[None, :])
    partial_out = jnp.dot(shaped, out_proj, preferred_element_type=f32).astype(bf16)
    summed = lax.psum_scatter(partial_out, "chan", scatter_dimension=1, tiled=True)
    channels = gate_gain.shape[0] * lax.axis_size("chan")
    norm_scale = lax.rsqrt(lax.psum(energy[:, 0], "chan") / channels + 1e-05)
    return (tokens.astype(f32) + summed.astype(f32) * norm_scale[:, None]).astype(bf16)


def solution(mesh):
    return jax.shard_map(
        local,
        mesh=mesh,
        in_specs=(
            P("seq", "chan"),
            P(),
            P(None, "chan"),
            P(None, "chan"),
            P("chan", None),
            P(None, "chan"),
            P(),
            P("chan"),
            P("chan"),
            P("chan"),
            P("chan"),
            P("chan", None),
        ),
        out_specs=P("seq", "chan"),
        check_vma=False,
    )
```

time: 429 us -> 281 us (0.66); the launches traced: 421 us -> 281 us
  waiting for transfers between devices: 232 us -> 134 us
  matrix products: 95.5 us -> 51.4 us
  Pallas kernels: 0 us -> 25.6 us
  local copies, waits for them, and re-layouts: 30.6 us -> 8.79 us
    reduce_scatter x1, waiting for transfers between devices: 116 us -> 55.6 us  [local(): lax.psum_scatter(partial_out, 'chan', scatter_dimension=1, tiled=True)]
    dot_general x9 -> x4, matrix products: 92 us -> 51.4 us  [the longest x1 14.8 us: local(): jnp.dot(normed, gate_proj, preferred_element_type=f32).astype(bf16)]
    pallas_call x0 -> x2, Pallas kernels: none -> 25.6 us  [the longest x1 18.7 us: local_scan(): pl.pallas_call(scan_kernel, grid=(rows // Q,), in_specs=[pl.BlockSpec((Q,...]
    reshape x4 -> x0, local copies, waits for them, and re-layouts: 21.4 us -> none  [the longest x2 15.7 us: local(): (local_out + carried_out).reshape(token_rows, heads * P_SIZE)]
    ppermute x5, waiting for transfers between devices: 28.7 us -> 9.09 us  [from_behind(): lax.ppermute(value, axis, [(source, source + steps) for source in range(l...]
    all_gather x2 -> x1, waiting for transfers between devices: 85.5 us -> 69.3 us  [local(): together = lax.all_gather(together, 'chan', axis=1, tiled=True)]
    mul x5 -> x0, other arithmetic: 8.02 us -> none  [the longest x2 4.48 us: causal_mix(): return jax.nn.silu(summed)]
    mul x3 -> x1, local copies, waits for them, and re-layouts: 5.47 us -> 0.07 us  [local(): fade_wide * carried.astype(f32) + device_end]
  transfers between devices with their start and end apart: 8 -> 7, of which waited for: 7 -> 4; matrix products, arithmetic and copies ran while one was open for 2% -> 13% of each run, Pallas kernels for 0% -> 0%
where the time goes in v1:
time: 281 us
  waiting for transfers between devices  134 us (48%)
  matrix products  51.4 us (18%)
  Pallas kernels  25.6 us (9%)
  starting transfers between devices  19.2 us (7%)
  other arithmetic  16.4 us (6%)
  between operations  13.6 us (5%)
  blocking collectives  11.8 us (4%)
  local copies, waits for them, and re-layouts  8.79 us (3%)
    all_gather x1, waiting for transfers between devices, local(): together = lax.all_gather(together, 'chan', axis=1, tiled=True)  69.3 us
    reduce_scatter x1, waiting for transfers between devices, local(): lax.psum_scatter(partial_out, 'chan', scatter_dimension=1, tiled=True)  55.6 us
    ppermute x5, starting transfers between devices, from_behind(): lax.ppermute(value, axis, [(source, source + steps) for source in range(l...  19.2 us
    pallas_call x1, Pallas kernels, local_scan(): pl.pallas_call(scan_kernel, grid=(rows // Q,), in_specs=[pl.BlockSpec((Q,...  18.7 us
    dot_general x1, matrix products, local(): jnp.dot(normed, gate_proj, preferred_element_type=f32).astype(bf16)  14.8 us
    dot_general x1, matrix products, local(): jnp.dot(shaped, out_proj, preferred_element_type=f32).astype(bf16)  14.7 us
    dot_general x1, matrix products, local(): jnp.dot(normed, inner_proj, preferred_element_type=f32).astype(bf16)  13.8 us
    psum x1, blocking collectives, local(): norm_scale = lax.rsqrt(lax.psum(energy[:, 0], 'chan') / channels + 1e-05)  11.8 us
  transfers between devices with their start and end apart: 7, of which 4 were waited for; matrix products, arithmetic and copies ran while one was open for 13% of the time, Pallas kernels for 0%

profile of v1, /device:TPU:0, one launch (start us, length us, event | category | flops | bytes accessed | tf_op | source)
XLA Modules:
  0.0 280.8 jit_solution(9829977296704900504)
XLA Ops:
  6.5 1.2 copy.17
  7.7 2.5 pad_maximum_fusion
  10.3 1.3 fusion.5
  11.5 0.7 copy.20.rate_t_ref
  12.2 0.7 broadcast_in_dim.21
  13.6 69.3 %all-gather.2.cloned.1.call-done = bf16[1408,4096]{1,0:T(8,128)(2,1)} async-done(((bf16[1408,512]{1,0:T(8,128)(2,1)}), bf16[1408,4096]{1,0:T(8,128)(2,1)}) %all-gather.2.cloned.1.call-update) | async-done | bytes 11534352 | tf_op jit(solution)/shard_map/all_gather | solution.py:222
  82.9 5.1 %fusion = f32[1024]{0:T(1024)S(1)} fusion(bf16[1408,4096]{1,0:T(8,128)(2,1)} %all-gather.2.cloned.1.call-done), kind=kLoop, calls=%fused_computation.2 | loop fusion | flops 12581888 | bytes 8392704 | tf_op jit(solution)/shard_map/reduce_sum | solution.py:225
  88.0 8.1 %fusion.3 = f32[1024,384]{1,0:T(8,128)S(1)} fusion(bf16[1408,4096]{1,0:T(8,128)(2,1)} %all-gather.2.cloned.1.call-done, f32[4096]{0:T(1024)S(1)} %copy-done.5, f32[1024]{0:T(1024)S(1)} %add_rsqrt_fusion.1), kind=kOutput, calls=%fused_computation.6 | convolution fusion | flops 3238002688 | bytes 13127680 | tf_op jit(solution)/shard_map/dot_general | solution.py:227
  96.1 3.4 %collective-permute-start.1 = (f32[8,256]{1,0:T(8,128)S(1)}, f32[8,256]{1,0:T(8,128)S(1)}, u32[]{:S(2)}, u32[]{:S(2)}) collective-permute-start(f32[8,256]{1,0:T(8,128)S(1)} %slice.25), channel_id=1, source_target_pairs={{0,8},{8,16},{16,24},{1,9},{9,17},{17,25},{2,10},{10,18},{18,26},{... | collective-permute-start | bytes 24584 | tf_op jit(solution)/shard_map/ppermute | solution.py:21
  99.9 13.8 %convolution_convert_fusion.2.inner_ref = bf16[1024,1024]{1,0:T(8,128)(2,1)S(1)} fusion(bf16[4096,1024]{1,0:T(8,128)(2,1)} %param.15, f32[4096]{0:T(1024)S(1)} %copy-done.5, f32[1024]{0:T(1024)S(1)} %add_rsqrt_fusion.1, bf16[1408,4096]{1,0:T(8,128)(2,1)} %all-gather.2.cloned.1.call-done), kind=kOutput, calls=%fused_computation.10 | convolution fusion | flops 8607760384 | bytes 18894848 | tf_op jit(solution)/shard_map/dot_general | solution.py:230
  113.7 3.6 %collective-permute-start = (bf16[8,1024]{1,0:T(8,128)(2,1)S(1)}, bf16[8,1024]{1,0:T(8,128)(2,1)S(1)}, u32[]{:S(2)}, u32[]{:S(2)}) collective-permute-start(bf16[8,1024]{1,0:T(8,128)(2,1)S(1)} %slice.22), channel_id=1, source_target_pairs={{0,8},{8,16},{16,24},{1,9},{9,17},{17,25},{2,10},{10,18},{18,26},{... | collective-permute-start | bytes 49160 | tf_op jit(solution)/shard_map/ppermute | solution.py:21
  117.3 0.7 fusion.14.step_t_ref
  118.2 1.1 slice.24.state_ref
  119.2 1.0 copy.19.step_ref
  121.4 18.7 %shard_map.118 = (f32[1024,1024]{1,0:T(8,128)}, bf16[1024,128]{1,0:T(8,128)(2,1)}, f32[1024,16]{1,0:T(8,128)}, f32[128,1024]{1,0:T(8,128)}, f32[1,16]{1,0:T(1,128)}) custom-call(bf16[1024,1024]{1,0:T(8,128)(2,1)} %copy-done.4, f32[8,1024]{1,0:T(8,128)} %convert_element_type.46.inner_rim_ref, f32[1024,256]{1,0:T(8,128)} %slice.24.state_ref, ...), custom_call_target="tpu_custom_call" | custom-call | flops 1073741824 | bytes 8388608 | tf_op jit(solution)/shard_map/pallas_call | solution.py:114
  140.1 1.1 convert_element_type.48
  141.2 3.4 %collective-permute-start.2 = (bf16[128,1024]{1,0:T(8,128)(2,1)S(1)}, bf16[128,1024]{1,0:T(8,128)(2,1)S(1)}, u32[]{:S(2)}, u32[]{:S(2)}) collective-permute-start(bf16[128,1024]{1,0:T(8,128)(2,1)S(1)} %convert_element_type.48), channel_id=1, source_target_pairs={{0,8},{8,16},{16,24},{1,9},{9,17},{17,25},{2,10},{10,18},{18,26},{... | collective-permute-start | bytes 786440 | tf_op jit(solution)/shard_map/ppermute | solution.py:21
  144.6 0.7 broadcast_in_dim.22
  145.4 4.6 %collective-permute-done.2 = bf16[128,1024]{1,0:T(8,128)(2,1)S(1)} collective-permute-done((bf16[128,1024]{1,0:T(8,128)(2,1)S(1)}, bf16[128,1024]{1,0:T(8,128)(2,1)S(1)}, u32[]{:S(2)}, u32[]{:S(2)}) %collective-permute-start.2) | collective-permute-done | bytes 262176 | tf_op jit(solution)/shard_map/ppermute | solution.py:21
  150.0 1.1 add_convert_fusion.2
  151.1 4.4 %collective-permute-start.3 = (bf16[128,1024]{1,0:T(8,128)(2,1)S(1)}, bf16[128,1024]{1,0:T(8,128)(2,1)S(1)}, u32[]{:S(2)}, u32[]{:S(2)}) collective-permute-start(bf16[128,1024]{1,0:T(8,128)(2,1)S(1)} %add_convert_fusion.2), channel_id=1, source_target_pairs={{0,8},{8,16},{16,24},{1,9},{9,17},{17,25},{2,10},{10,18},{18,26},{... | collective-permute-start | bytes 786440 | tf_op jit(solution)/shard_map/ppermute | solution.py:21
  155.5 4.5 %collective-permute-done.3 = bf16[128,1024]{1,0:T(8,128)(2,1)S(1)} collective-permute-done((bf16[128,1024]{1,0:T(8,128)(2,1)S(1)}, bf16[128,1024]{1,0:T(8,128)(2,1)S(1)}, u32[]{:S(2)}, u32[]{:S(2)}) %collective-permute-start.3) | collective-permute-done | bytes 262176 | tf_op jit(solution)/shard_map/ppermute | solution.py:21
  160.0 1.1 add_convert_fusion.1
  161.2 4.4 %collective-permute-start.4 = (bf16[128,1024]{1,0:T(8,128)(2,1)S(1)}, bf16[128,1024]{1,0:T(8,128)(2,1)S(1)}, u32[]{:S(2)}, u32[]{:S(2)}) collective-permute-start(bf16[128,1024]{1,0:T(8,128)(2,1)S(1)} %add_convert_fusion.1), channel_id=1, source_target_pairs={{0,8},{8,16},{16,24},{1,9},{9,17},{17,25},{2,10},{10,18},{18,26},{... | collective-permute-start | bytes 786440 | tf_op jit(solution)/shard_map/ppermute | solution.py:21
  165.6 14.8 %convolution_convert_fusion.1.gate_ref = bf16[1024,1024]{1,0:T(8,128)(2,1)} fusion(bf16[4096,1024]{1,0:T(8,128)(2,1)} %param.14, f32[4096]{0:T(1024)S(1)} %copy-done.5, f32[1024]{0:T(1024)S(1)} %add_rsqrt_fusion.1, bf16[1408,4096]{1,0:T(8,128)(2,1)} %all-gather.2.cloned.1.call-done), kind=kOutput, calls=%fused_computation.9 | convolution fusion | flops 8607760384 | bytes 18894848 | tf_op jit(solution)/shard_map/dot_general | solution.py:231
  180.4 0.7 copy-done.2
  181.1 6.9 %shard_map.119 = (bf16[1024,1024]{1,0:T(8,128)(2,1)}, f32[1024,1]{1,0:T(8,128)}) custom-call(f32[1024,1024]{1,0:T(8,128)} %get-tuple-element.12.y_ref, bf16[1024,1024]{1,0:T(8,128)(2,1)} %convolution_convert_fusion.1.gate_ref, bf16[1024,128]{1,0:T(8,128)(2,1)} %get-tuple-element.13.out_map_ref, f32[1024,16]{1,0:T(8,128)} %get-tuple-element.14.log_ref, ...), custom_call_target="tpu_custom_call" | custom-call | flops 268435456 | bytes 8388608 | tf_op jit(solution)/shard_map/pallas_call | solution.py:183
  188.0 14.7 %convolution_convert_fusion = bf16[1024,4096]{1,0:T(8,128)(2,1)} fusion(bf16[1024,1024]{1,0:T(8,128)(2,1)} %get-tuple-element.17, bf16[1024,4096]{1,0:T(8,128)(2,1)} %param.23), kind=kOutput, calls=%fused_computation.5 | convolution fusion | flops 8594128896 | bytes 18874368 | tf_op jit(solution)/shard_map/dot_general | solution.py:249
  202.7 1.0 copy-done.1
  203.9 11.8 %psum.7 = f32[1024]{0:T(1024)S(1)} all-reduce(f32[1024]{0:T(1024)S(1)} %reduce), channel_id=1, replica_groups=mesh['seq'=4,'chan'=8] {'chan'}, use_global_device_ids=true, to_apply=%region_2.3 | all-reduce | flops 1024 | bytes 8192 | tf_op jit(solution)/shard_map/psum | solution.py:252
  215.8 55.6 %reduce-scatter.2.cloned.1.call-done = bf16[1024,512]{1,0:T(8,128)(2,1)} async-done(((bf16[1024,4096]{1,0:T(8,128)(2,1)}), bf16[1024,512]{1,0:T(8,128)(2,1)}) %reduce-scatter.2.cloned.1.call-update) | async-done | bytes 1048592 | tf_op jit(solution)/shard_map/reduce_scatter | solution.py:250
  271.4 2.6 add_convert_fusion
  (30 shorter events, 2.7 us)
Async XLA Ops:
  6.5 81.4 %copy-start.5 = (f32[4096]{0:T(1024)S(1)}, f32[4096]{0:T(1024)}, u32[]{:S(2)}) copy-start(f32[4096]{0:T(1024)} %param.13) | copy-start | bytes 49156
  6.5 76.4 %all-gather.2.cloned.1.call-start = ((), (), s32[]{:S(2)}) async-start(), calls=%async_computation.1 | async-start | bytes 12976128 | tf_op jit(solution)/shard_map/all_gather | solution.py:222
  10.2 261.2 %reduce-scatter.2.cloned.1.call-start = ((), (), s32[]{:S(2)}) async-start(), calls=%async_computation.2 | async-start | bytes 9437184 | tf_op jit(solution)/shard_map/reduce_scatter | solution.py:250
  96.1 24.7 %collective-permute-start.1 = (f32[8,256]{1,0:T(8,128)S(1)}, f32[8,256]{1,0:T(8,128)S(1)}, u32[]{:S(2)}, u32[]{:S(2)}) collective-permute-start(f32[8,256]{1,0:T(8,128)S(1)} %slice.25), channel_id=1, source_target_pairs={{0,8},{8,16},{16,24},{1,9},{9,17},{17,25},{2,10},{10,18},{18,26},{... | collective-permute-start | bytes 24584 | tf_op jit(solution)/shard_map/ppermute | solution.py:21
  99.9 17.4 %copy-start.3 = (f32[16]{0:T(128)S(1)}, f32[16]{0:T(128)}, u32[]{:S(2)}) copy-start(f32[16]{0:T(128)} %param.20) | copy-start | bytes 196
  113.7 4.5 %copy-start.4 = (bf16[1024,1024]{1,0:T(8,128)(2,1)}, bf16[1024,1024]{1,0:T(8,128)(2,1)S(1)}, u32[]{:S(2)}) copy-start(bf16[1024,1024]{1,0:T(8,128)(2,1)S(1)} %convolution_convert_fusion.2.inner_ref) | copy-start | bytes 6291460
  113.7 6.5 %collective-permute-start = (bf16[8,1024]{1,0:T(8,128)(2,1)S(1)}, bf16[8,1024]{1,0:T(8,128)(2,1)S(1)}, u32[]{:S(2)}, u32[]{:S(2)}) collective-permute-start(bf16[8,1024]{1,0:T(8,128)(2,1)S(1)} %slice.22), channel_id=1, source_target_pairs={{0,8},{8,16},{16,24},{1,9},{9,17},{17,25},{2,10},{10,18},{18,26},{... | collective-permute-start | bytes 49160 | tf_op jit(solution)/shard_map/ppermute | solution.py:21
  120.8 0.6 copy-start.6
  141.2 8.8 %collective-permute-start.2 = (bf16[128,1024]{1,0:T(8,128)(2,1)S(1)}, bf16[128,1024]{1,0:T(8,128)(2,1)S(1)}, u32[]{:S(2)}, u32[]{:S(2)}) collective-permute-start(bf16[128,1024]{1,0:T(8,128)(2,1)S(1)} %convert_element_type.48), channel_id=1, source_target_pairs={{0,8},{8,16},{16,24},{1,9},{9,17},{17,25},{2,10},{10,18},{18,26},{... | collective-permute-start | bytes 786440 | tf_op jit(solution)/shard_map/ppermute | solution.py:21
  151.1 8.9 %collective-permute-start.3 = (bf16[128,1024]{1,0:T(8,128)(2,1)S(1)}, bf16[128,1024]{1,0:T(8,128)(2,1)S(1)}, u32[]{:S(2)}, u32[]{:S(2)}) collective-permute-start(bf16[128,1024]{1,0:T(8,128)(2,1)S(1)} %add_convert_fusion.2), channel_id=1, source_target_pairs={{0,8},{8,16},{16,24},{1,9},{9,17},{17,25},{2,10},{10,18},{18,26},{... | collective-permute-start | bytes 786440 | tf_op jit(solution)/shard_map/ppermute | solution.py:21
  161.2 19.2 %collective-permute-start.4 = (bf16[128,1024]{1,0:T(8,128)(2,1)S(1)}, bf16[128,1024]{1,0:T(8,128)(2,1)S(1)}, u32[]{:S(2)}, u32[]{:S(2)}) collective-permute-start(bf16[128,1024]{1,0:T(8,128)(2,1)S(1)} %add_convert_fusion.1), channel_id=1, source_target_pairs={{0,8},{8,16},{16,24},{1,9},{9,17},{17,25},{2,10},{10,18},{18,26},{... | collective-permute-start | bytes 786440 | tf_op jit(solution)/shard_map/ppermute | solution.py:21
  180.4 0.7 copy-start.2
  202.7 1.0 copy-start.1
  202.7 68.7 %copy-start = (bf16[1024,512]{1,0:T(8,128)(2,1)S(1)}, bf16[1024,512]{1,0:T(8,128)(2,1)}, u32[]{:S(2)}) copy-start(bf16[1024,512]{1,0:T(8,128)(2,1)} %param.12) | copy-start | bytes 3145732
Sparse Core Ops, SparseCore 0:
  10.3 72.5 all-gather.1
  202.8 68.5 reduce-scatter.1

commit v2 on v1

--- a/solution.py
+++ b/solution.py
@@ -11,6 +11,7 @@
 Q = 256
 LANES = 2 * P_SIZE
 RIM = 8
+ROWS = 128
 
 f32, bf16 = jnp.float32, jnp.bfloat16
 
@@ -157,8 +158,9 @@
     )
 
 
-def finish_kernel(y_ref, gate_ref, out_map_ref, log_ref, carried_ref, gain_ref, shaped_ref, energy_ref):
+def finish_kernel(y_ref, gate_ref, late_gate_ref, out_map_ref, log_ref, carried_ref, gain_ref, shaped_ref, energy_ref):
     heads = log_ref.shape[1]
+    early = pl.program_id(0) < pl.num_programs(0) // 2
     grown = jnp.exp(log_ref[...])
     out_map = out_map_ref[...]
     energy = jnp.zeros((Q, LANES), f32)
@@ -166,16 +168,17 @@
         lanes = slice(pair * LANES, (pair + 1) * LANES)
         carried = jnp.dot(out_map, carried_ref[:, lanes], preferred_element_type=f32)
         y = y_ref[:, lanes] + carried * wide_pair(grown, pair)
-        gate = gate_ref[:, lanes].astype(f32)
+        gate = jnp.where(early, gate_ref[:, lanes].astype(f32), late_gate_ref[:, lanes].astype(f32))
         gated = y * (gate * (1.0 / (1.0 + jnp.exp(-gate))))
         energy = energy + gated * gated
         shaped_ref[:, lanes] = (gated * gain_ref[:, lanes]).astype(bf16)
     energy_ref[...] = jnp.sum(energy, axis=1, keepdims=True)
 
 
-def finish(y, gate_raw, out_map, logs, carried, gate_gain):
+def finish(y, gates, out_map, logs, carried, gate_gain):
     rows, width = y.shape
     heads = logs.shape[1]
+    middle = rows // Q // 2
 
     def rowwise(columns):
         return pl.BlockSpec((Q, columns), lambda c: (c, 0))
@@ -185,7 +188,8 @@
         grid=(rows // Q,),
         in_specs=[
             rowwise(width),
-            rowwise(width),
+            pl.BlockSpec((Q, width), lambda c: (jnp.minimum(c, middle - 1), 0)),
+            pl.BlockSpec((Q, width), lambda c: (jnp.maximum(c - middle, 0), 0)),
             rowwise(N),
             rowwise(heads),
             pl.BlockSpec((N, width), lambda c: (0, 0)),
@@ -200,7 +204,48 @@
         cost_estimate=pl.CostEstimate(
             flops=rows * width * N * 2, bytes_accessed=rows * width * 8, transcendentals=rows * width
         ),
-    )(y, gate_raw, out_map, logs, carried, gate_gain)
+    )(y, gates[0], gates[1], out_map, logs, carried, gate_gain)
+
+
+def norm_kernel(token_ref, state_proj_ref, gain_ref, normed_ref, projected_ref):
+    widened = token_ref[...].astype(f32)
+    square = jnp.mean(widened * widened, axis=1, keepdims=True)
+    normed = (widened * lax.rsqrt(square + 1e-05) * gain_ref[...]).astype(bf16)
+    normed_ref[...] = normed
+    projected_ref[...] = lax.dot_general(
+        normed, state_proj_ref[...], (((1,), (1,)), ((), ())), preferred_element_type=f32
+    )
+
+
+def norm_and_project(together, norm_gain, outputs):
+    width = together.shape[1]
+    rows = together.shape[0] - outputs
+    skipped = outputs // ROWS
+    return pl.pallas_call(
+        norm_kernel,
+        grid=(rows // ROWS,),
+        in_specs=[
+            pl.BlockSpec((ROWS, width), lambda c: (c + skipped, 0)),
+            pl.BlockSpec((outputs, width), lambda c: (0, 0)),
+            pl.BlockSpec((1, width), lambda c: (0, 0)),
+        ],
+        out_specs=[
+            pl.BlockSpec((ROWS, width), lambda c: (c, 0)),
+            pl.BlockSpec((ROWS, outputs), lambda c: (c, 0)),
+        ],
+        out_shape=[
+            jax.ShapeDtypeStruct((rows, width), bf16),
+            jax.ShapeDtypeStruct((rows, outputs), f32),
+        ],
+        compiler_params=pltpu.CompilerParams(dimension_semantics=("arbitrary",)),
+        cost_estimate=pl.CostEstimate(
+            flops=rows * width * outputs * 2, bytes_accessed=rows * width * 4, transcendentals=rows
+        ),
+    )(together, together, norm_gain[None, :])
+
+
+def gate_part(normed, gate_proj, start, rows):
+    return jnp.dot(normed[start : start + rows], gate_proj, preferred_element_type=f32).astype(bf16)
 
 
 def local(
@@ -218,17 +263,11 @@
     out_proj,
 ):
     token_rows = tokens.shape[0]
-    together = jnp.concatenate([tokens, state_proj.T], axis=0)
+    outputs = state_proj.shape[1]
+    together = jnp.concatenate([state_proj.T, tokens], axis=0)
     together = lax.all_gather(together, "chan", axis=1, tiled=True)
-    gathered, state_proj_t = together[:token_rows], together[token_rows:]
-    widened = gathered.astype(f32)
-    inverse = lax.rsqrt(jnp.mean(widened * widened, axis=1, keepdims=True) + 1e-05)
-    normed = (widened * inverse * norm_gain).astype(bf16)
-    projected = lax.dot_general(
-        normed, state_proj_t, (((1,), (1,)), ((), ())), preferred_element_type=f32
-    )
+    normed, projected = norm_and_project(together, norm_gain, outputs)
     inner_raw = jnp.dot(normed, inner_proj, preferred_element_type=f32).astype(bf16)
-    gate_raw = jnp.dot(normed, gate_proj, preferred_element_type=f32).astype(bf16)
     heads = log_rate.shape[0]
     start_head = lax.axis_index("chan") * heads
     state_raw = projected[:, : 2 * N]
@@ -242,10 +281,19 @@
         conv_inner, conv_state, skip_wide,
     )
     fade_wide = jnp.repeat(device_fade[0], P_SIZE)[None, :]
+    hops = lax.axis_size("seq") - 1
+    half = token_rows // 2
+    gates = []
     carried = from_behind(device_end.astype(bf16), "seq", 1)
-    for _ in range(lax.axis_size("seq") - 2):
-        carried = from_behind((fade_wide * carried.astype(f32) + device_end).astype(bf16), "seq", 1)
-    shaped, energy = finish(y, gate_raw, out_map, logs, carried, gate_gain[None, :])
+    for hop in range(1, hops):
+        onward = (fade_wide * carried.astype(f32) + device_end).astype(bf16)
+        if hop >= hops - 1:
+            gates.append(gate_part(normed, gate_proj, 0, half))
+            onward, gates[0] = lax.optimization_barrier((onward, gates[0]))
+        carried = from_behind(onward, "seq", 1)
+    while len(gates) < 2:
+        gates.append(gate_part(normed, gate_proj, len(gates) * half, half))
+    shaped, energy = finish(y, gates, out_map, logs, carried, gate_gain[None, :])
     partial_out = jnp.dot(shaped, out_proj, preferred_element_type=f32).astype(bf16)
     summed = lax.psum_scatter(partial_out, "chan", scatter_dimension=1, tiled=True)
     channels = gate_gain.shape[0] * lax.axis_size("chan")

time: 281 us -> 279 us (level)
  Pallas kernels: 25.6 us -> 38.7 us
  matrix products: 51.4 us -> 44.2 us
  other arithmetic: 16.4 us -> 9.74 us
    pallas_call x0 -> x1, Pallas kernels: none -> 13.2 us  [norm_and_project(): pl.pallas_call(norm_kernel, grid=(rows // ROWS,), in_specs=[pl.BlockSpec(...]
    dot_general x2, matrix products: 22.9 us -> 15.7 us  [gate_part(): jnp.dot(normed[start:start + rows], gate_proj, preferred_element_type=f32)]
    reduce_sum x1 -> x0, other arithmetic: 5.07 us -> none  [local(): jnp.mean(widened * widened, axis=1, keepdims=True) + 1e-05]
    ppermute x5, waiting for transfers between devices: 9.09 us -> 4.65 us  [from_behind(): lax.ppermute(value, axis, [(source, source + steps) for source in range(l...]
  transfers between devices with their start and end apart: 7 -> 7, of which waited for: 4 -> 3; matrix products, arithmetic and copies ran while one was open for 13% -> 8% of each run, Pallas kernels for 0% -> 0%
where the time goes in v2:
time: 279 us; the launch traced here: 278 us
  waiting for transfers between devices  132 us (47%)
  matrix products  44.2 us (16%)
  Pallas kernels  38.7 us (14%)
  starting transfers between devices  18.1 us (6%)
  between operations  13.6 us (5%)
  blocking collectives  11.8 us (4%)
  local copies, waits for them, and re-layouts  10.3 us (4%)
  other arithmetic  9.74 us (3%)
    all_gather x1, waiting for transfers between devices, local(): together = lax.all_gather(together, 'chan', axis=1, tiled=True)  70.7 us
    reduce_scatter x1, waiting for transfers between devices, local(): lax.psum_scatter(partial_out, 'chan', scatter_dimension=1, tiled=True)  56.3 us
    pallas_call x1, Pallas kernels, local_scan(): pl.pallas_call(scan_kernel, grid=(rows // Q,), in_specs=[pl.BlockSpec((Q,...  18.7 us
    ppermute x5, starting transfers between devices, from_behind(): lax.ppermute(value, axis, [(source, source + steps) for source in range(l...  18.1 us
    dot_general x2, matrix products, gate_part(): jnp.dot(normed[start:start + rows], gate_proj, preferred_element_type=f32)  15.7 us
    dot_general x1, matrix products, local(): jnp.dot(shaped, out_proj, preferred_element_type=f32).astype(bf16)  14.8 us
    dot_general x1, matrix products, local(): jnp.dot(normed, inner_proj, preferred_element_type=f32).astype(bf16)  13.8 us
    pallas_call x1, Pallas kernels, norm_and_project(): pl.pallas_call(norm_kernel, grid=(rows // ROWS,), in_specs=[pl.BlockSpec(...  13.2 us
  transfers between devices with their start and end apart: 7, of which 3 were waited for; matrix products, arithmetic and copies ran while one was open for 8% of the time, Pallas kernels for 0%

profile of v2, /device:TPU:0, one launch (start us, length us, event | category | flops | bytes accessed | tf_op | source)
XLA Modules:
  0.0 278.3 jit_solution(11826838039708718827)
XLA Ops:
  6.5 1.2 copy.17
  7.7 2.5 pad_maximum_fusion
  10.9 0.7 copy.20.rate_t_ref
  11.7 0.7 broadcast_in_dim_reshape.4.skip_ref
  12.3 70.7 %all-gather.2.cloned.1.call-done.token_ref.state_proj_ref = bf16[1408,4096]{1,0:T(8,128)(2,1)} async-done(((bf16[1408,512]{1,0:T(8,128)(2,1)}), bf16[1408,4096]{1,0:T(8,128)(2,1)}) %all-gather.2.cloned.1.call-update) | async-done | bytes 11534352 | tf_op jit(solution)/shard_map/all_gather | solution.py:268
  83.0 13.2 %shard_map.118 = (bf16[1024,4096]{1,0:T(8,128)(2,1)}, f32[1024,384]{1,0:T(8,128)}) custom-call(bf16[1408,4096]{1,0:T(8,128)(2,1)} %all-gather.2.cloned.1.call-done.token_ref.state_proj_ref, bf16[1408,4096]{1,0:T(8,128)(2,1)} %all-gather.2.cloned.1.call-done.token_ref.state_proj_ref, f32[1,4096]{1,0:T(1,128)} %bitcast.17), custom_call_target="tpu_custom_call" | custom-call | flops 3221225472 | bytes 16777216 | tf_op jit(solution)/shard_map/pallas_call | solution.py:224
  96.2 0.7 slice.18
  96.9 1.9 copy.18
  98.8 13.8 %convolution_convert_fusion.1.inner_ref = bf16[1024,1024]{1,0:T(8,128)(2,1)S(1)} fusion(bf16[1024,4096]{1,0:T(8,128)(2,1)} %get-tuple-element.16, bf16[4096,1024]{1,0:T(8,128)(2,1)} %param.15), kind=kOutput, calls=%fused_computation.6 | convolution fusion | flops 8590983168 | bytes 18874368 | tf_op jit(solution)/shard_map/dot_general | solution.py:270
  112.6 3.4 %collective-permute-start = (bf16[8,1024]{1,0:T(8,128)(2,1)S(1)}, bf16[8,1024]{1,0:T(8,128)(2,1)S(1)}, u32[]{:S(2)}, u32[]{:S(2)}) collective-permute-start(bf16[8,1024]{1,0:T(8,128)(2,1)S(1)} %slice.21), channel_id=1, source_target_pairs={{0,8},{8,16},{16,24},{1,9},{9,17},{17,25},{2,10},{10,18},{18,26},{... | collective-permute-start | bytes 49160 | tf_op jit(solution)/shard_map/ppermute | solution.py:22
  116.0 3.4 %collective-permute-start.1 = (f32[8,256]{1,0:T(8,128)S(1)}, f32[8,256]{1,0:T(8,128)S(1)}, u32[]{:S(2)}, u32[]{:S(2)}) collective-permute-start(f32[8,256]{1,0:T(8,128)S(1)} %slice.18), channel_id=1, source_target_pairs={{0,8},{8,16},{16,24},{1,9},{9,17},{17,25},{2,10},{10,18},{18,26},{... | collective-permute-start | bytes 24584 | tf_op jit(solution)/shard_map/ppermute | solution.py:22
  119.6 0.7 fusion.18.step_t_ref
  120.3 1.1 slice.17.state_ref
  121.4 1.0 copy.19.step_ref
  122.4 0.6 convert_element_type.41.inner_rim_ref
  123.6 18.7 %shard_map.119 = (f32[1024,1024]{1,0:T(8,128)}, bf16[1024,128]{1,0:T(8,128)(2,1)}, f32[1024,16]{1,0:T(8,128)}, f32[128,1024]{1,0:T(8,128)}, f32[1,16]{1,0:T(1,128)}) custom-call(bf16[1024,1024]{1,0:T(8,128)(2,1)} %copy-done.7, f32[8,1024]{1,0:T(8,128)} %convert_element_type.41.inner_rim_ref, f32[1024,256]{1,0:T(8,128)} %slice.17.state_ref, ...), custom_call_target="tpu_custom_call" | custom-call | flops 1073741824 | bytes 8388608 | tf_op jit(solution)/shard_map/pallas_call | solution.py:115
  142.3 1.1 convert_element_type.42
  143.4 3.4 %collective-permute-start.2 = (bf16[128,1024]{1,0:T(8,128)(2,1)S(1)}, bf16[128,1024]{1,0:T(8,128)(2,1)S(1)}, u32[]{:S(2)}, u32[]{:S(2)}) collective-permute-start(bf16[128,1024]{1,0:T(8,128)(2,1)S(1)} %convert_element_type.42), channel_id=1, source_target_pairs={{0,8},{8,16},{16,24},{1,9},{9,17},{17,25},{2,10},{10,18},{18,26},{... | collective-permute-start | bytes 786440 | tf_op jit(solution)/shard_map/ppermute | solution.py:22
  146.8 0.7 broadcast_in_dim.24
  147.5 4.6 %collective-permute-done.2 = bf16[128,1024]{1,0:T(8,128)(2,1)S(1)} collective-permute-done((bf16[128,1024]{1,0:T(8,128)(2,1)S(1)}, bf16[128,1024]{1,0:T(8,128)(2,1)S(1)}, u32[]{:S(2)}, u32[]{:S(2)}) %collective-permute-start.2) | collective-permute-done | bytes 262176 | tf_op jit(solution)/shard_map/ppermute | solution.py:22
  152.2 1.3 add_convert_fusion.2
  153.5 4.8 %collective-permute-start.3 = (bf16[128,1024]{1,0:T(8,128)(2,1)S(1)}, bf16[128,1024]{1,0:T(8,128)(2,1)S(1)}, u32[]{:S(2)}, u32[]{:S(2)}) collective-permute-start(bf16[128,1024]{1,0:T(8,128)(2,1)S(1)} %add_convert_fusion.2), channel_id=1, source_target_pairs={{0,8},{8,16},{16,24},{1,9},{9,17},{17,25},{2,10},{10,18},{18,26},{... | collective-permute-start | bytes 786440 | tf_op jit(solution)/shard_map/ppermute | solution.py:22
  158.3 10.1 %fusion.4.gate_ref = bf16[512,1024]{1,0:T(8,128)(2,1)} fusion(bf16[4096,1024]{1,0:T(8,128)(2,1)} %param.14, bf16[1024,4096]{1,0:T(8,128)(2,1)} %get-tuple-element.16), kind=kOutput, calls=%fused_computation.7 | convolution fusion | flops 4295491584 | bytes 13631488 | tf_op jit(solution)/shard_map/dot_general | solution.py:248
  168.5 3.1 %collective-permute-start.4 = (bf16[128,1024]{1,0:T(8,128)(2,1)S(1)}, bf16[128,1024]{1,0:T(8,128)(2,1)S(1)}, u32[]{:S(2)}, u32[]{:S(2)}) collective-permute-start(bf16[128,1024]{1,0:T(8,128)(2,1)S(1)} %add_convert_fusion.1), channel_id=1, source_target_pairs={{0,8},{8,16},{16,24},{1,9},{9,17},{17,25},{2,10},{10,18},{18,26},{... | collective-permute-start | bytes 786440 | tf_op jit(solution)/shard_map/ppermute | solution.py:22
  171.7 5.6 %fusion.7.late_gate_ref = bf16[512,1024]{1,0:T(8,128)(2,1)} fusion(bf16[4096,1024]{1,0:T(8,128)(2,1)S(1)} %bitcast.21, bf16[1024,4096]{1,0:T(8,128)(2,1)S(1)} %bitcast.23), kind=kOutput, calls=%fused_computation.8 | convolution fusion | flops 4295491584 | bytes 13631488 | tf_op jit(solution)/shard_map/dot_general | solution.py:248
  177.2 0.7 copy-done.4
  177.9 6.7 %shard_map.120 = (bf16[1024,1024]{1,0:T(8,128)(2,1)}, f32[1024,1]{1,0:T(8,128)}) custom-call(f32[1024,1024]{1,0:T(8,128)} %get-tuple-element.18.y_ref, bf16[512,1024]{1,0:T(8,128)(2,1)} %fusion.4.gate_ref, bf16[512,1024]{1,0:T(8,128)(2,1)} %fusion.7.late_gate_ref, bf16[1024,128]{1,0:T(8,128)(2,1)} %get-tuple-element.22.out_map_ref, ...), custom_call_target="tpu_custom_call" | custom-call | flops 268435456 | bytes 8388608 | tf_op jit(solution)/shard_map/pallas_call | solution.py:186
  184.7 14.8 %convolution_convert_fusion = bf16[1024,4096]{1,0:T(8,128)(2,1)} fusion(bf16[1024,1024]{1,0:T(8,128)(2,1)} %get-tuple-element.25, bf16[1024,4096]{1,0:T(8,128)(2,1)} %param.23), kind=kOutput, calls=%fused_computation | convolution fusion | flops 8594128896 | bytes 18874368 | tf_op jit(solution)/shard_map/dot_general | solution.py:297
  199.4 1.0 copy-done.3
  200.7 11.8 %psum.7 = f32[1024]{0:T(1024)S(1)} all-reduce(f32[1024]{0:T(1024)S(1)} %reduce), channel_id=1, replica_groups=mesh['seq'=4,'chan'=8] {'chan'}, use_global_device_ids=true, to_apply=%region_1.2 | all-reduce | flops 1024 | bytes 8192 | tf_op jit(solution)/shard_map/psum | solution.py:300
  212.5 56.3 %reduce-scatter.2.cloned.1.call-done = bf16[1024,512]{1,0:T(8,128)(2,1)} async-done(((bf16[1024,4096]{1,0:T(8,128)(2,1)}), bf16[1024,512]{1,0:T(8,128)(2,1)}) %reduce-scatter.2.cloned.1.call-update) | async-done | bytes 1048592 | tf_op jit(solution)/shard_map/reduce_scatter | solution.py:298
  268.9 2.6 add_convert_fusion
  (44 shorter events, 1.9 us)
Async XLA Ops:
  6.5 3.8 %copy-start.9 = (f32[16]{0:T(128)S(1)}, f32[16]{0:T(128)}, u32[]{:S(2)}) copy-start(f32[16]{0:T(128)} %param.19) | copy-start | bytes 196
  6.5 5.1 %copy-start.6 = (f32[16]{0:T(128)S(1)}, f32[16]{0:T(128)}, u32[]{:S(2)}) copy-start(f32[16]{0:T(128)} %param.21) | copy-start | bytes 196
  6.5 76.5 %all-gather.2.cloned.1.call-start = ((), (), s32[]{:S(2)}) async-start(), calls=%async_computation.1 | async-start | bytes 12976128 | tf_op jit(solution)/shard_map/all_gather | solution.py:268
  10.3 258.6 %reduce-scatter.2.cloned.1.call-start = ((), (), s32[]{:S(2)}) async-start(), calls=%async_computation.2 | async-start | bytes 9437184 | tf_op jit(solution)/shard_map/reduce_scatter | solution.py:298
  98.8 20.6 %copy-start.5 = (f32[16]{0:T(128)S(1)}, f32[16]{0:T(128)}, u32[]{:S(2)}) copy-start(f32[16]{0:T(128)} %param.20) | copy-start | bytes 196
  98.8 21.5 %copy-start.1 = (f32[1024,384]{1,0:T(8,128)S(1)}, f32[1024,384]{1,0:T(8,128)}, u32[]{:S(2)}) copy-start(f32[1024,384]{1,0:T(8,128)} %get-tuple-element.17) | copy-start | bytes 4718596
  112.6 7.7 %copy-start.7 = (bf16[1024,1024]{1,0:T(8,128)(2,1)}, bf16[1024,1024]{1,0:T(8,128)(2,1)S(1)}, u32[]{:S(2)}) copy-start(bf16[1024,1024]{1,0:T(8,128)(2,1)S(1)} %convolution_convert_fusion.1.inner_ref) | copy-start | bytes 6291460
  112.6 9.7 %collective-permute-start = (bf16[8,1024]{1,0:T(8,128)(2,1)S(1)}, bf16[8,1024]{1,0:T(8,128)(2,1)S(1)}, u32[]{:S(2)}, u32[]{:S(2)}) collective-permute-start(bf16[8,1024]{1,0:T(8,128)(2,1)S(1)} %slice.21), channel_id=1, source_target_pairs={{0,8},{8,16},{16,24},{1,9},{9,17},{17,25},{2,10},{10,18},{18,26},{... | collective-permute-start | bytes 49160 | tf_op jit(solution)/shard_map/ppermute | solution.py:22
  116.0 6.9 %collective-permute-start.1 = (f32[8,256]{1,0:T(8,128)S(1)}, f32[8,256]{1,0:T(8,128)S(1)}, u32[]{:S(2)}, u32[]{:S(2)}) collective-permute-start(f32[8,256]{1,0:T(8,128)S(1)} %slice.18), channel_id=1, source_target_pairs={{0,8},{8,16},{16,24},{1,9},{9,17},{17,25},{2,10},{10,18},{18,26},{... | collective-permute-start | bytes 24584 | tf_op jit(solution)/shard_map/ppermute | solution.py:22
  123.0 0.6 copy-start.8
  143.4 8.8 %collective-permute-start.2 = (bf16[128,1024]{1,0:T(8,128)(2,1)S(1)}, bf16[128,1024]{1,0:T(8,128)(2,1)S(1)}, u32[]{:S(2)}, u32[]{:S(2)}) collective-permute-start(bf16[128,1024]{1,0:T(8,128)(2,1)S(1)} %convert_element_type.42), channel_id=1, source_target_pairs={{0,8},{8,16},{16,24},{1,9},{9,17},{17,25},{2,10},{10,18},{18,26},{... | collective-permute-start | bytes 786440 | tf_op jit(solution)/shard_map/ppermute | solution.py:22
  152.2 19.4 %slice-start = ((s8[8388608]{0:T(1024)(128)(4,1)}), s8[4194304]{0:T(1024)(128)(4,1)S(1)}, s32[]{:S(2)}) async-start(s8[8388608]{0:T(1024)(128)(4,1)} %bitcast.20), calls=%async_computation.3 | async-start | bytes 8388608
  152.2 19.4 %slice-start.2 = ((s8[8388608]{0:T(1024)(128)(4,1)}), s8[4194304]{0:T(1024)(128)(4,1)S(1)}, s32[]{:S(2)}) async-start(s8[8388608]{0:T(1024)(128)(4,1)} %bitcast.22), calls=%async_computation.5 | async-start | bytes 8388608
  153.4 15.0 %copy-start = (f32[128,1024]{1,0:T(8,128)S(1)}, f32[128,1024]{1,0:T(8,128)}, u32[]{:S(2)}) copy-start(f32[128,1024]{1,0:T(8,128)} %get-tuple-element.20) | copy-start | bytes 1572868
  153.5 18.2 %slice-start.1 = ((s8[8388608]{0:T(1024)(128)(4,1)}), s8[4194304]{0:T(1024)(128)(4,1)S(1)}, s32[]{:S(2)}) async-start(s8[8388608]{0:T(1024)(128)(4,1)} %bitcast.20), calls=%async_computation.4 | async-start | bytes 8388608
  153.5 18.2 %slice-start.3 = ((s8[8388608]{0:T(1024)(128)(4,1)}), s8[4194304]{0:T(1024)(128)(4,1)S(1)}, s32[]{:S(2)}) async-start(s8[8388608]{0:T(1024)(128)(4,1)} %bitcast.22), calls=%async_computation.6 | async-start | bytes 8388608
  153.5 15.0 %collective-permute-start.3 = (bf16[128,1024]{1,0:T(8,128)(2,1)S(1)}, bf16[128,1024]{1,0:T(8,128)(2,1)S(1)}, u32[]{:S(2)}, u32[]{:S(2)}) collective-permute-start(bf16[128,1024]{1,0:T(8,128)(2,1)S(1)} %add_convert_fusion.2), channel_id=1, source_target_pairs={{0,8},{8,16},{16,24},{1,9},{9,17},{17,25},{2,10},{10,18},{18,26},{... | collective-permute-start | bytes 786440 | tf_op jit(solution)/shard_map/ppermute | solution.py:22
  168.5 8.7 %collective-permute-start.4 = (bf16[128,1024]{1,0:T(8,128)(2,1)S(1)}, bf16[128,1024]{1,0:T(8,128)(2,1)S(1)}, u32[]{:S(2)}, u32[]{:S(2)}) collective-permute-start(bf16[128,1024]{1,0:T(8,128)(2,1)S(1)} %add_convert_fusion.1), channel_id=1, source_target_pairs={{0,8},{8,16},{16,24},{1,9},{9,17},{17,25},{2,10},{10,18},{18,26},{... | collective-permute-start | bytes 786440 | tf_op jit(solution)/shard_map/ppermute | solution.py:22
  177.2 0.7 copy-start.4
  199.4 1.0 copy-start.3
  199.4 69.4 %copy-start.2 = (bf16[1024,512]{1,0:T(8,128)(2,1)S(1)}, bf16[1024,512]{1,0:T(8,128)(2,1)}, u32[]{:S(2)}) copy-start(bf16[1024,512]{1,0:T(8,128)(2,1)} %param.12) | copy-start | bytes 3145732
Sparse Core Ops, SparseCore 0:
  10.4 72.5 all-gather.1
  199.6 69.2 reduce-scatter.1
